TPU v7x, 32 devices: a whole 2x2x4 slice. The times are simulated.
32 devices in a mesh: bra: 8 (over z, x), ket: 2 (over y), mpo: 2 (over core).
Axes of the slice: x: 2, y: 2, z: 4, core: 2. Of those that a mesh axis runs over, the one named last changes fastest.
Arguments:
- left_env: bfloat16 [4, 3072, 3072], P('mpo', 'bra', 'ket'), may hold values from -6 to 6
- site_tensor: bfloat16 [3072, 4, 3072], P('bra', None, 'ket'), may hold values from -0.0546875 to 0.0546875
- block_values: float32 [12, 4, 4], replicated, may hold values from -3 to 3
- pair_in: int32 [12], replicated, may hold values from 0 to 3
- pair_out: int32 [12], replicated, may hold values from 0 to 3, as said below
Outputs:
- new_env: bfloat16 [4, 3072, 3072], P('mpo', 'bra', 'ket')
Inputs may be any that keep to these rules, and one draw needn't show every extreme that they name: `pair_out`: every component number 0 to 3 appears at least once.
All inputs are finite; a program needn't handle non-finite values.
Results may differ from a plain program's by a relative error of at most 0.018.
Values may be sent and summed in bfloat16 or wider, within the bound.
A program may use at most 192 MiB of HBM per device.

v0:
```python
import jax
import jax.numpy as jnp
from jax import lax
from jax.sharding import PartitionSpec as P

K = 4


def local(left_env, site_tensor, block_values, pair_in, pair_out):
    comps_loc = left_env.shape[0]
    rows_loc = left_env.shape[1]
    cols_loc = left_env.shape[2]
    phys = site_tensor.shape[1]
    comps = jnp.arange(K, dtype=jnp.int32)
    hot_out = (pair_out[:, None] == comps[None, :]).astype(jnp.float32)
    hot_in = (pair_in[:, None] == comps[None, :]).astype(jnp.float32)
    mixing = jnp.einsum(
        "pv,pw,pst->vswt", hot_out, hot_in, block_values, precision=lax.Precision.HIGHEST
    )
    splits = lax.axis_size("mpo")
    half_cols = cols_loc // splits
    own_start = lax.axis_index("mpo") * half_cols
    site_own = lax.dynamic_slice_in_dim(site_tensor, own_start, half_cols, 2)
    site_full = lax.all_gather(
        site_own.reshape(rows_loc, phys * half_cols), "bra", axis=0, tiled=True
    )
    piece = lax.all_gather(left_env, "ket", axis=2, tiled=True)
    piece = lax.all_gather(piece, "mpo", axis=0, tiled=True)
    comps_all, width = piece.shape[0], piece.shape[2]
    half = jnp.dot(
        piece.reshape(comps_all * rows_loc, width), site_full, preferred_element_type=jnp.float32
    )
    half = half.astype(jnp.bfloat16).reshape(comps_all, rows_loc, phys, half_cols)
    mixed = jnp.einsum(
        "vswt,watc->savc", mixing, half.astype(jnp.float32), precision=lax.Precision.HIGHEST
    ).astype(jnp.bfloat16)
    mixed_pairs = mixed.reshape(phys * rows_loc, comps_all * half_cols)
    site_wide = lax.all_gather(
        jnp.transpose(site_tensor, (1, 0, 2)), "ket", axis=2, tiled=True
    )
    site_pairs = site_wide.reshape(phys * rows_loc, site_wide.shape[2])
    term = lax.dot_general(
        site_pairs, mixed_pairs, (((0,), (0,)), ((), ())), preferred_element_type=jnp.float32
    ).astype(jnp.bfloat16)
    owned = lax.psum_scatter(term, "bra", scatter_dimension=0, tiled=True)
    owned = jnp.transpose(owned.reshape(-1, comps_all, half_cols), (1, 0, 2))
    return lax.all_to_all(owned, "mpo", split_axis=0, concat_axis=2, tiled=True)


def solution(mesh):
    return jax.shard_map(
        local,
        mesh=mesh,
        in_specs=(P("mpo", "bra", "ket"), P("bra", None, "ket"), P(), P(), P()),
        out_specs=P("mpo", "bra", "ket"),
        check_vma=False,
    )
```

profile of v0, /device:TPU:12, one launch (start us, length us, event | category | flops | bytes accessed | tf_op | source)
XLA Modules:
  0.0 975.3 jit_solution(10487822228750793544)
XLA Ops:
  6.5 0.0 all-gather.7.cloned.1.call-start
  6.5 0.7 all-gather.7.cloned.1.call-update
  7.3 0.0 all-gather.9.cloned.1.call-start
  7.3 64.4 %all-gather.7.cloned.1.call-done = bf16[2,384,3072]{2,1,0:T(8,128)(2,1)} async-done(((bf16[2,384,1536]{2,1,0:T(8,128)(2,1)}), bf16[2,384,3072]{2,1,0:T(8,128)(2,1)}) %all-gather.7.cloned.1.call-update) | async-done | bytes 4718608 | tf_op jit(solution)/shard_map/all_gather | solution.py:27
  71.7 0.0 all-gather.9.cloned.1.call-update
  71.8 0.0 all-gather.5.cloned.1.call-start
  71.8 2.5 constant_dynamic-slice_fusion
  74.3 1.9 copy.27
  76.2 0.0 copy-start.1
  76.2 0.0 copy-start.2
  76.2 0.0 copy-start
  76.2 0.0 all-gather.5.cloned.1.call-update
  76.2 0.0 all-gather.11.cloned.1.call-start
  76.3 5.7 copy.34
  81.9 0.0 all-gather.11.cloned.1.call-update
  82.0 0.0 reduce-scatter.4.cloned.1.call-start
  82.0 0.0 copy-done.1
  82.0 0.0 copy-done.2
  82.0 0.0 copy-done
  82.1 0.3 convolution_bitcast_fusion
  82.4 13.7 %all-gather.9.cloned.1.call-done = bf16[4,384,3072]{2,1,0:T(8,128)(2,1)} async-done(((bf16[2,384,3072]{2,1,0:T(8,128)(2,1)}), bf16[4,384,3072]{2,1,0:T(8,128)(2,1)}) %all-gather.9.cloned.1.call-update) | async-done | bytes 9437200 | tf_op jit(solution)/shard_map/all_gather | solution.py:28
  96.1 364.8 %all-gather.5.cloned.1.call-done = bf16[3072,3072]{1,0:T(8,128)(2,1)} async-done(((bf16[384,3072]{1,0:T(8,128)(2,1)}), bf16[3072,3072]{1,0:T(8,128)(2,1)}) %all-gather.5.cloned.1.call-update) | async-done | bytes 18874384 | tf_op jit(solution)/shard_map/all_gather | solution.py:24
  461.0 36.7 %fusion = bf16[1536,3072]{0,1:T(8,128)(2,1)} fusion(bf16[3072,3072]{1,0:T(8,128)(2,1)} %all-gather.5.cloned.1.call-done, bf16[1536,3072]{1,0:T(8,128)(2,1)} %bitcast.57), kind=kOutput, calls=%fused_computation.3 | convolution fusion | flops 28995747840 | bytes 37748736 | tf_op jit(solution)/shard_map/dot_general | solution.py:30
  497.7 16.5 %reshape.22 = bf16[4,384,4,768]{1,0,3,2:T(4,128)(2,1)} reshape(bf16[1536,3072]{0,1:T(8,128)(2,1)} %fusion) | data formatting | bytes 18874368 | tf_op jit(solution)/shard_map/reshape | solution.py:33
  514.1 19.3 %copy.19 = bf16[4,384,4,768,1]{3,0,2,4,1:T(4,128)(2,1)} copy(bf16[4,384,4,768,1]{1,0,3,2,4:T(4,128)(2,1)} %bitcast.48) | data formatting | bytes 18874368 | tf_op jit(solution)/shard_map/reshape | solution.py:33
  533.4 20.1 %fusion.1 = bf16[4,384,4,768]{3,0,2,1:T(4,128)(2,1)S(1)} fusion(bf16[4,384,4,768,1]{3,0,2,4,1:T(4,128)(2,1)} %copy.19, f32[4,4,4,4,1]{1,2,3,0,4:T(4,128)S(1)} %convolution_bitcast_fusion), kind=kOutput, calls=%fused_computation.4 | convolution fusion | flops 910688256 | bytes 18875392 | tf_op jit(solution)/shard_map/vswt,watc->savc/dot_general | solution.py:34
  553.5 6.2 copy.15
  559.8 9.6 copy.28
  569.3 10.1 %all-gather.11.cloned.1.call-done = bf16[4,384,3072]{2,1,0:T(8,128)(2,1)} async-done(((bf16[4,384,1536]{2,1,0:T(8,128)(2,1)}), bf16[4,384,3072]{2,1,0:T(8,128)(2,1)}) %all-gather.11.cloned.1.call-update) | async-done | bytes 9437200 | tf_op jit(solution)/shard_map/all_gather | solution.py:38
  579.5 36.8 %convert_bitcast_fusion = bf16[3072,3072]{0,1:T(8,128)(2,1)} fusion(bf16[1536,3072]{1,0:T(8,128)(2,1)} %bitcast.51, bf16[1536,3072]{1,0:T(8,128)(2,1)} %bitcast.58), kind=kOutput, calls=%fused_computation.1 | convolution fusion | flops 29000466432 | bytes 37748736 | tf_op jit(solution)/shard_map/dot_general | solution.py:42
  616.2 24.6 %copy.25 = bf16[3072,3072]{1,0:T(8,128)(2,1)} copy(bf16[3072,3072]{0,1:T(8,128)(2,1)} %convert_bitcast_fusion) | data formatting | bytes 37748736
  640.8 0.0 reduce-scatter.4.cloned.1.call-update
  640.9 309.6 %reduce-scatter.4.cloned.1.call-done = bf16[384,3072]{1,0:T(8,128)(2,1)} async-done(((bf16[3072,3072]{1,0:T(8,128)(2,1)}), bf16[384,3072]{1,0:T(8,128)(2,1)}) %reduce-scatter.4.cloned.1.call-update) | async-done | bytes 2359312
  950.5 3.0 copy.26
  953.5 6.5 all_to_all.18
  960.0 6.0 copy.17
  966.0 2.8 all_to_all.16
  (1 shorter events, 0.0 us)
Async XLA Ops:
  6.5 65.2 %all-gather.7.cloned.1.call-start = ((), (), s32[]{:S(2)}) async-start(), calls=%async_computation.3 | async-start | bytes 7077888 | tf_op jit(solution)/shard_map/all_gather | solution.py:27
  7.3 88.9 %all-gather.9.cloned.1.call-start = ((), (), s32[]{:S(2)}) async-start(), calls=%async_computation.4 | async-start | bytes 14155776 | tf_op jit(solution)/shard_map/all_gather | solution.py:28
  71.8 389.2 %all-gather.5.cloned.1.call-start = ((), (), s32[]{:S(2)}) async-start(), calls=%async_computation.2 | async-start | bytes 21233664 | tf_op jit(solution)/shard_map/all_gather | solution.py:24
  76.2 5.8 copy-start.1
  76.2 5.8 copy-start.2
  76.2 5.9 copy-start
  76.2 503.3 %all-gather.11.cloned.1.call-start = ((), (), s32[]{:S(2)}) async-start(), calls=%async_computation.5 | async-start | bytes 14155776 | tf_op jit(solution)/shard_map/all_gather | solution.py:38
  82.0 868.5 %reduce-scatter.4.cloned.1.call-start = ((), (), s32[]{:S(2)}) async-start(), calls=%async_computation.6 | async-start | bytes 21233664
Sparse Core Ops, SparseCore 0:
  8.9 62.8 all-gather.6
  73.3 22.8 all-gather.8
  97.7 363.2 all-gather.4
  462.4 117.0 all-gather.10
  641.0 309.4 reduce-scatter.3
where the time goes:
time: 980 us; the launch traced here: 975 us
  waiting for transfers between devices  764 us (78%)
  local copies, waits for them, and re-layouts  97.9 us (10%)
  matrix products  93.9 us (10%)
  between operations  13.2 us (1%)
    all_gather x1, waiting for transfers between devices, local(): lax.all_gather(site_own.reshape(rows_loc, phys * half_cols), 'bra', axis=...  365 us
    unnamed x6, waiting for transfers between devices  310 us
    all_gather x1, waiting for transfers between devices, local(): piece = lax.all_gather(left_env, 'ket', axis=2, tiled=True)  64.4 us
    unnamed x11, local copies, waits for them, and re-layouts  44.7 us
    dot_general x1, matrix products, local(): lax.dot_general(site_pairs, mixed_pairs, (((0,), (0,)), ((), ())), prefer...  36.8 us
    dot_general x1, matrix products, local(): jnp.dot(piece.reshape(comps_all * rows_loc, width), site_full, preferred_...  36.7 us
    reshape x2, local copies, waits for them, and re-layouts, local(): half.astype(jnp.bfloat16).reshape(comps_all, rows_loc, phys, half_cols)  35.7 us
    dot_general x1, matrix products, local(): jnp.einsum('vswt,watc->savc', mixing, half.astype(jnp.float32), precision...  20.1 us
  transfers between devices with their start and end apart: 5, of which 5 were waited for; matrix products, arithmetic and copies ran while one was open for 12% of the time, Pallas kernels for 0%

commit v1 on v0

v1 whole, which is shorter than its diff:
```python
import functools

import jax
import jax.numpy as jnp
from jax import lax
from jax.experimental import pallas as pl
from jax.experimental.pallas import tpu as pltpu
from jax.sharding import PartitionSpec as P

K = 4
LANES = 128
MESH = pl.DeviceIdType.MESH
BF16 = jnp.bfloat16
F32 = jnp.float32


def mixing_of(block_values, pair_in, pair_out):
    comps = jnp.arange(K, dtype=jnp.int32)
    hot_out = (pair_out[:, None] == comps[None, :]).astype(F32)
    hot_in = (pair_in[:, None] == comps[None, :]).astype(F32)
    return jnp.einsum(
        "pv,pw,pst->vswt", hot_out, hot_in, block_values, precision=lax.Precision.HIGHEST
    )


def plain(left_env, site_tensor, block_values, pair_in, pair_out):
    rows_loc = left_env.shape[1]
    cols_loc = left_env.shape[2]
    phys = site_tensor.shape[1]
    mixing = mixing_of(block_values, pair_in, pair_out)
    splits = lax.axis_size("mpo")
    half_cols = cols_loc // splits
    own_start = lax.axis_index("mpo") * half_cols
    site_own = lax.dynamic_slice_in_dim(site_tensor, own_start, half_cols, 2)
    site_full = lax.all_gather(
        site_own.reshape(rows_loc, phys * half_cols), "bra", axis=0, tiled=True
    )
    piece = lax.all_gather(left_env, "ket", axis=2, tiled=True)
    piece = lax.all_gather(piece, "mpo", axis=0, tiled=True)
    comps_all, width = piece.shape[0], piece.shape[2]
    half = jnp.dot(
        piece.reshape(comps_all * rows_loc, width), site_full, preferred_element_type=F32
    )
    half = half.astype(BF16).reshape(comps_all, rows_loc, phys, half_cols)
    mixed = jnp.einsum(
        "vswt,watc->savc", mixing, half.astype(F32), precision=lax.Precision.HIGHEST
    ).astype(BF16)
    mixed_pairs = mixed.reshape(phys * rows_loc, comps_all * half_cols)
    site_wide = lax.all_gather(
        jnp.transpose(site_tensor, (1, 0, 2)), "ket", axis=2, tiled=True
    )
    site_pairs = site_wide.reshape(phys * rows_loc, site_wide.shape[2])
    term = lax.dot_general(
        site_pairs, mixed_pairs, (((0,), (0,)), ((), ())), preferred_element_type=F32
    ).astype(BF16)
    owned = lax.psum_scatter(term, "bra", scatter_dimension=0, tiled=True)
    owned = jnp.transpose(owned.reshape(-1, comps_all, half_cols), (1, 0, 2))
    return lax.all_to_all(owned, "mpo", split_axis=0, concat_axis=2, tiled=True)


def update_kernel(
    nz, nj, rows, phys,
    l_ref, a_ref, c_ref, mk_ref,
    out_ref, up_ref, down_ref,
    env, conj, cols, half, terms, stage, total,
    own_sem, xy_send, xy_recv, col_send, col_recv, z_send, z_recv,
    up_send, up_recv, down_send, down_recv, stage_sem, fin_send, fin_recv, fin_own,
):
    bra, y, k = lax.axis_index("bra"), lax.axis_index("ket"), lax.axis_index("mpo")
    z, x = bra // 2, lax.rem(bra, 2)
    xo, yo, ko = 1 - x, 1 - y, 1 - k
    xn, yn, kn = (z * 2 + xo, y, k), (bra, yo, k), (bra, y, ko)
    xkn = (z * 2 + xo, y, ko)
    zu, zd = (bra + 2, y, k), (bra - 2, y, k)
    has_up, has_down = z < nz - 1, z > 0
    width = phys * LANES
    part = rows // 2

    barrier = pltpu.get_barrier_semaphore()
    for device in (xn, yn, kn, xkn):
        pl.semaphore_signal(barrier, inc=1, device_id=device, device_id_type=MESH)

    @pl.when(has_up)
    def _():
        pl.semaphore_signal(barrier, inc=1, device_id=zu, device_id_type=MESH)

    @pl.when(has_down)
    def _():
        pl.semaphore_signal(barrier, inc=1, device_id=zd, device_id_type=MESH)

    pl.semaphore_wait(barrier, 4 + (z + nz - 1) // nz + (2 * nz - 2 - z) // nz)

    def remote(src, dst, send, recv, device):
        return pltpu.make_async_remote_copy(
            src_ref=src, dst_ref=dst, send_sem=send, recv_sem=recv,
            device_id=device, device_id_type=MESH,
        )

    def slot(q, xs, ys, ks, h):
        if q == 0:
            return env.at[ys, xs, ks, h]
        return conj.at[2 * ys + lax.rem(h + ys, 2), xs, ks]

    def own(q, h):
        return l_ref.at[h] if q == 0 else a_ref.at[lax.rem(h + y, 2), k]

    upper, lower = pl.ds(0, part), pl.ds(part, part)

    def xy(q, h, t, receiving):
        ks = ko if receiving else k
        if t == 0:
            dst = slot(q, xo if receiving else x, y, k, h)
            src, device = own(q, h), xn
        elif t == 1:
            dst = slot(q, x, yo if receiving else y, k, h)
            src, device = own(q, h), yn
        elif t == 2:
            dst = slot(q, xo if receiving else x, yo, k, h).at[lower]
            src, device = dst, xn
        elif t == 3:
            dst = slot(q, xo, yo if receiving else y, k, h).at[upper]
            src, device = dst, yn
        else:
            dst = slot(q, xo if t in (5, 7) else x, yo if t in (6, 7) else y, ks, h)
            src, device = own(q, h) if t == 4 else dst, kn
        if receiving:
            src = dst
        return remote(src, dst, xy_send.at[q, h, t], xy_recv.at[q, h, t], device)

    def xy_start(q, h, t):
        xy(q, h, t, False).start()

    def xy_wait(q, h, t):
        xy(q, h, t, True).wait_recv()

    def from_x(q, h):
        xy_wait(q, h, 0)
        xy_start(q, h, 3)
        xy_start(q, h, 5)

    def from_y(q, h):
        xy_wait(q, h, 1)
        xy_start(q, h, 2)
        xy_start(q, h, 6)

    def diagonal(q, h):
        xy_wait(q, h, 2)
        xy_wait(q, h, 3)
        xy_start(q, h, 7)

    def from_core(q, h):
        for t in range(4 if q == 0 else 5, 8):
            xy_wait(q, h, t)

    def col_rows(index, count):
        return pl.ds(pl.multiple_of(index * rows, rows), count * rows)

    def col(j, receiving):
        dst = cols.at[j, col_rows(z * 2 + (xo if receiving else x), 1)]
        return remote(c_ref.at[xo, k, j], dst, col_send.at[j], col_recv.at[j], xn)

    def hop(j, up, s, receiving):
        piece = (z - s if receiving else z - s + 1) if up else (z + s if receiving else z + s - 1)
        ref = cols.at[j, col_rows(piece * 2, 2)]
        way = 0 if up else 1
        return remote(
            ref, ref, z_send.at[j, way, s - 1], z_recv.at[j, way, s - 1], zu if up else zd
        )

    def hop_sends(up, s):
        return (has_up & (z >= s - 1)) if up else (has_down & (z <= nz - s))

    def hop_start(j, s):
        for up in (True, False):
            @pl.when(hop_sends(up, s))
            def _():
                hop(j, up, s, False).start()

    def hop_sent(j):
        for s in range(1, nz):
            for up in (True, False):
                @pl.when(hop_sends(up, s))
                def _():
                    hop(j, up, s, False).wait_send()

    def hop_pass(j, s):
        for up in (True, False):
            @pl.when((z >= s) if up else (z < nz - s))
            def _():
                hop(j, up, s, True).wait_recv()

            if s < nz - 1:
                @pl.when(hop_sends(up, s + 1))
                def _():
                    hop(j, up, s + 1, False).start()

    deep = nz * rows

    def first_product(j):
        def body(i, carry):
            xs, ks = i // 2, lax.rem(i, 2)
            acc = jnp.dot(
                env[0, xs, ks].reshape(2 * rows, deep), cols[j, :deep], preferred_element_type=F32
            )
            acc += jnp.dot(
                env[1, xs, ks].reshape(2 * rows, deep), cols[j, deep:], preferred_element_type=F32
            )
            half[xs, pl.ds(2 * ks, 2)] = acc.astype(BF16).reshape(2, rows, width)
            return carry

        lax.fori_loop(0, 4, body, 0)

    group = 4
    span = group * 16

    def mix(j):
        per_x = rows // span

        def body(i, carry):
            xs, base = i // per_x, pl.multiple_of(lax.rem(i, per_x) * span, span)
            tiles = [
                half[xs, w, pl.ds(base, span), t * LANES:(t + 1) * LANES]
                for w in range(K) for t in range(phys)
            ]
            right = jnp.concatenate(
                [
                    jnp.concatenate([tile[g * 16:(g + 1) * 16] for tile in tiles], axis=0)
                    for g in range(group)
                ],
                axis=1,
            )
            both = jnp.dot(mk_ref[...], right, preferred_element_type=F32)
            size = K * phys * 16
            result = (both[:size] + both[size:]).astype(BF16)
            for v in range(K):
                for s in range(phys):
                    row = (v * phys + s) * 16
                    for g in range(group):
                        at = pl.multiple_of(xs * deep + s * rows + base + g * 16, 16)
                        cols[j, pl.ds(at, 16), v * LANES:(v + 1) * LANES] = result[
                            row:row + 16, g * LANES:(g + 1) * LANES
                        ]
            return carry

        lax.fori_loop(0, 2 * per_x, body, 0)

    def term_ref(j, d):
        if j < 2:
            return terms.at[j, d]
        return env.at[d // 2, d % 2, 0, :, :, pl.ds((j - 2) * width, width)]

    def up_copy(j, d):
        return remote(term_ref(j, d), up_ref.at[j, d], up_send.at[j, d], up_recv.at[j, d], zu)

    def down_copy(j, d):
        return remote(
            term_ref(j, d), down_ref.at[j, d], down_send.at[j, d], down_recv.at[j, d], zd
        )

    def second_product(j, d):
        out = term_ref(j, d)
        acc = jnp.dot(
            conj[d, 0].reshape(2 * rows, deep), cols[j, :deep], preferred_element_type=F32
        )
        acc += jnp.dot(
            conj[d, 1].reshape(2 * rows, deep), cols[j, deep:], preferred_element_type=F32
        )
        out[...] = acc.astype(BF16).reshape(2, rows, width)
        if d > 0:
            @pl.when(z == 0)
            def _():
                up_copy(j, d).start()
        if d < nz - 1:
            @pl.when(z == nz - 1)
            def _():
                down_copy(j, d).start()

    strip = 96
    strips = rows // strip

    def strip_of(i):
        return i // strips, pl.ds(pl.multiple_of(lax.rem(i, strips) * strip, strip), strip)

    def fetch(src, index):
        return pltpu.make_async_copy(src, stage.at[index], stage_sem.at[index])

    def pass_on(j, d, up):
        copy = up_copy(j, d) if up else down_copy(j, d)
        copy.wait_recv()
        local = fetch((up_ref if up else down_ref).at[j, d], 0)
        local.start()
        local.wait()
        ref = term_ref(j, d)

        def body(i, carry):
            b, r = strip_of(i)
            ref[b, r] = (ref[b, r].astype(F32) + stage[0, b, r].astype(F32)).astype(BF16)
            return carry

        lax.fori_loop(0, 2 * strips, body, 0)
        copy.start()

    def fin(j, t, receiving):
        xs, ks, device = ((x, ko, kn), (xo, k, xn), (xo, ko, xkn))[t]
        block = (xs * 2 + ks) if receiving else (x * 2 + k)
        dst = out_ref.at[
            :, :, pl.ds(pl.multiple_of((block * nj + j) * LANES, LANES), LANES)
        ]
        src = total.at[j, pl.ds(2 * ks, 2), pl.ds(pl.multiple_of(xs * rows, rows), rows)]
        return remote(src, dst, fin_send.at[j, t], fin_recv.at[j, t], device)

    def fin_local(j):
        dst = out_ref.at[
            :, :, pl.ds(pl.multiple_of(((x * 2 + k) * nj + j) * LANES, LANES), LANES)
        ]
        src = total.at[j, pl.ds(2 * k, 2), pl.ds(pl.multiple_of(x * rows, rows), rows)]
        return pltpu.make_async_copy(src, dst, fin_own.at[j])

    def finish(j, d):
        below, above = d > 0, d < nz - 1
        count = 0
        for there, copy, src in ((below, up_copy, up_ref), (above, down_copy, down_ref)):
            if there:
                copy(j, d).wait_recv()
                fetch(src.at[j, d], count).start()
                count += 1
        for index in range(count):
            fetch(up_ref.at[j, d], index).wait()
        ref = term_ref(j, d)

        def body(i, carry):
            b, r = strip_of(i)
            value = ref[b, r].astype(F32)
            for index in range(count):
                value += stage[index, b, r].astype(F32)
            value = value.astype(BF16)
            at = pl.ds(pl.multiple_of(i * strip, strip), strip)
            for v in range(K):
                total[j, v, at] = value[:, v * LANES:(v + 1) * LANES]
            return carry

        lax.fori_loop(0, 2 * strips, body, 0)
        for t in range(3):
            fin(j, t, False).start()
        fin_local(j).start()

    for j in range(nj):
        col(j, False).start()
    for h in range(2):
        xy_start(0, h, 0)
        xy_start(0, h, 1)
        xy_start(0, h, 4)

    def col_own(j):
        return pltpu.make_async_copy(
            c_ref.at[x, k, j], cols.at[j, col_rows(z * 2 + x, 1)], own_sem.at[0, j]
        )

    env_own = [
        pltpu.make_async_copy(l_ref.at[h], env.at[y, x, k, h], own_sem.at[1, h]) for h in range(2)
    ]
    conj_own = [
        pltpu.make_async_copy(a_ref.at[h], conj.at[2 * y + h, x], own_sem.at[2, h])
        for h in range(2)
    ]
    for j in range(nj):
        col_own(j).start()
    for copy in env_own + conj_own:
        copy.start()

    for j in range(nj):
        col_own(j).wait()
        col(j, True).wait_recv()
        hop_start(j, 1)
    from_y(0, 0)
    hop_pass(0, 1)
    for j in range(1, nj):
        hop_pass(j, 1)
        if j == 1:
            from_y(0, 1)
            from_x(0, 0)
    from_x(0, 1)
    xy_start(1, 0, 0)
    xy_start(1, 0, 1)
    hop_pass(0, 2)
    diagonal(0, 0)
    diagonal(0, 1)
    for j in range(1, nj):
        hop_pass(j, 2)
    for copy in env_own + conj_own:
        copy.wait()
    from_core(0, 0)
    from_core(0, 1)
    from_y(1, 0)
    from_x(1, 0)
    xy_start(1, 1, 0)
    xy_start(1, 1, 1)

    def product_and_mix(j):
        hop_pass(j, 3)
        first_product(j)
        hop_sent(j)
        mix(j)

    far = (nz - 1, 0)
    near = tuple(d for d in range(nz - 1, -1, -1) if d not in far)
    product_and_mix(0)
    product_and_mix(1)
    diagonal(1, 0)
    from_core(1, 0)
    for j in range(2):
        for d in far:
            second_product(j, d)
    from_y(1, 1)
    from_x(1, 1)
    for j in range(2, nj):
        product_and_mix(j)
    diagonal(1, 1)
    from_core(1, 1)
    for h in range(2):
        for t in range(8):
            xy(0, h, t, False).wait_send()
    for j in range(2):
        for d in near:
            second_product(j, d)
    for j in range(2, nj):
        for d in far + near:
            second_product(j, d)
    order = [(j, d) for j in range(2) for d in far] + [(j, d) for j in range(2) for d in near]
    order += [(j, d) for j in range(2, nj) for d in far + near]
    for own_z in range(nz):
        @pl.when(z == own_z)
        def _():
            for j, d in order:
                d = d if 2 * own_z < nz else nz - 1 - d
                if d == own_z:
                    finish(j, d)
                elif d > own_z and own_z > 0:
                    pass_on(j, d, True)
                elif d < own_z and own_z < nz - 1:
                    pass_on(j, d, False)
            for j, d in order:
                if d > own_z:
                    up_copy(j, d).wait_send()
                elif d < own_z:
                    down_copy(j, d).wait_send()

    for j in range(nj):
        col(j, False).wait_send()
        fin_local(j).wait()
        for t in range(3):
            fin(j, t, False).wait_send()
            fin(j, t, True).wait_recv()
    for h in range(2):
        for t in (0, 1, 2, 3, 5, 6, 7):
            xy(1, h, t, False).wait_send()


def fused(nz, left_env, site_tensor, block_values, pair_in, pair_out):
    rows, phys, width_loc = site_tensor.shape
    nj = width_loc // (4 * LANES)
    mixing = mixing_of(block_values, pair_in, pair_out).reshape(K * phys, K * phys)
    high = lax.reduce_precision(mixing, 8, 7)
    eye = jnp.eye(16, dtype=F32)
    spread = jnp.concatenate([jnp.kron(high, eye), jnp.kron(mixing - high, eye)], axis=0)
    spread = spread.astype(BF16)
    columns = site_tensor.reshape(rows, phys, 2, 2, nj, LANES)
    columns = columns.transpose(2, 3, 4, 0, 1, 5).reshape(2, 2, nj, rows, phys * LANES)
    turned = site_tensor.transpose(2, 1, 0).reshape(2, 2, rows, phys * rows)
    width = phys * LANES
    dma = pltpu.SemaphoreType.DMA
    anywhere = pl.BlockSpec(memory_space=pl.ANY)
    out, _, _ = pl.pallas_call(
        functools.partial(update_kernel, nz, nj, rows, phys),
        out_shape=(
            jax.ShapeDtypeStruct(left_env.shape, BF16),
            jax.ShapeDtypeStruct((nj, nz, 2, rows, width), BF16),
            jax.ShapeDtypeStruct((nj, nz, 2, rows, width), BF16),
        ),
        in_specs=[anywhere, anywhere, anywhere, pl.BlockSpec(memory_space=pltpu.VMEM)],
        out_specs=(anywhere, anywhere, anywhere),
        scratch_shapes=[
            pltpu.VMEM((2, 2, 2, 2, rows, width_loc), BF16),
            pltpu.VMEM((nz, 2, 2, rows, phys * rows), BF16),
            pltpu.VMEM((nj, 2 * nz * rows, width), BF16),
            pltpu.VMEM((2, K, rows, width), BF16),
            pltpu.VMEM((2, nz, 2, rows, width), BF16),
            pltpu.VMEM((2, 2, rows, width), BF16),
            pltpu.VMEM((nj, K, 2 * rows, LANES), BF16),
            dma((3, max(nj, 2))),
            dma((2, 2, 8)), dma((2, 2, 8)),
            dma((nj,)), dma((nj,)),
            dma((nj, 2, nz - 1)), dma((nj, 2, nz - 1)),
            dma((nj, nz)), dma((nj, nz)),
            dma((nj, nz)), dma((nj, nz)),
            dma((2,)),
            dma((nj, 3)), dma((nj, 3)), dma((nj,)),
        ],
        compiler_params=pltpu.CompilerParams(
            collective_id=0, has_side_effects=True, vmem_limit_bytes=67043328
        ),
    )(left_env, turned, columns, spread)
    return out


def solution(mesh):
    sizes = dict(mesh.shape)

    def local(left_env, site_tensor, block_values, pair_in, pair_out):
        comps_loc = left_env.shape[0]
        rows, phys, width = site_tensor.shape
        fits = (
            sizes["ket"] == 2 and sizes["mpo"] == 2 and sizes["bra"] == 8
            and comps_loc == 2 and phys == 4 and rows % 192 == 0
            and width == (sizes["bra"] // 2) * rows and width % (4 * LANES) == 0
            and 2 <= width // (4 * LANES) <= 3 and rows <= 384
        )
        if fits:
            return fused(
                sizes["bra"] // 2, left_env, site_tensor, block_values, pair_in, pair_out
            )
        return plain(left_env, site_tensor, block_values, pair_in, pair_out)

    return jax.shard_map(
        local,
        mesh=mesh,
        in_specs=(P("mpo", "bra", "ket"), P("bra", None, "ket"), P(), P(), P()),
        out_specs=P("mpo", "bra", "ket"),
        check_vma=False,
    )
```

time: 980 us -> 411 us (0.42)
  waiting for transfers between devices: 764 us -> 0 us
  Pallas kernels: 0 us -> 357 us
  matrix products: 93.9 us -> 1.03 us
  local copies, waits for them, and re-layouts: 97.9 us -> 49.6 us
  between operations: 13.2 us -> 0.04 us
    all_gather x4 -> x0, waiting for transfers between devices: 453 us -> none  [the longest x1 365 us: local(): lax.all_gather(site_own.reshape(rows_loc, phys * half_cols), 'bra', axis=...]
    pallas_call x0 -> x1, Pallas kernels: none -> 357 us  [fused(): pl.pallas_call(functools.partial(update_kernel, nz, nj, rows, phys), out_...]
    unnamed x6 -> x0, waiting for transfers between devices: 310 us -> none
    dot_general x4 -> x1, matrix products: 93.9 us -> 1.03 us  [mixing_of(): jnp.einsum('pv,pw,pst->vswt', hot_out, hot_in, block_values, precision=la...]
    unnamed x11 -> x2, local copies, waits for them, and re-layouts: 44.7 us -> 12.2 us
    reshape x2 -> x3, local copies, waits for them, and re-layouts: 35.7 us -> 16.9 us  [the longest x1 8.76 us: fused(): turned = site_tensor.transpose(2, 1, 0).reshape(2, 2, rows, phys * rows)]
    transpose x0 -> x3, local copies, waits for them, and re-layouts: none -> 18.6 us  [the longest x1 10.2 us: fused(): turned = site_tensor.transpose(2, 1, 0).reshape(2, 2, rows, phys * rows)]
  transfers between devices with their start and end apart: 5 -> 0, of which waited for: 5 -> 0; matrix products, arithmetic and copies ran while one was open for 12% -> 0% of each run, Pallas kernels for 0% -> 0%
where the time goes in v1:
time: 411 us; the launch traced here: 409 us
  Pallas kernels  357 us (87%)
  local copies, waits for them, and re-layouts  49.6 us (12%)
    pallas_call x1, Pallas kernels, fused(): pl.pallas_call(functools.partial(update_kernel, nz, nj, rows, phys), out_...  357 us
    unnamed x2, local copies, waits for them, and re-layouts  12.2 us
    transpose x1, local copies, waits for them, and re-layouts, fused(): turned = site_tensor.transpose(2, 1, 0).reshape(2, 2, rows, phys * rows)  10.2 us
    reshape x1, local copies, waits for them, and re-layouts, fused(): turned = site_tensor.transpose(2, 1, 0).reshape(2, 2, rows, phys * rows)  8.76 us
    transpose x1, local copies, waits for them, and re-layouts, fused(): columns.transpose(2, 3, 4, 0, 1, 5).reshape(2, 2, nj, rows, phys * LANES)  8.39 us

profile of v1, /device:TPU:12, one launch (start us, length us, event | category | flops | bytes accessed | tf_op | source)
XLA Modules:
  0.0 409.2 jit_solution(8772230311721414243)
XLA Ops:
  0.0 0.7 fusion.6
  0.7 1.0 convolution_bitcast_fusion
  1.7 0.1 reshape.48
  1.8 0.4 multiply_convert_fusion.1
  2.2 1.0 mul.44
  3.2 1.0 mul.47
  4.2 0.7 pad_maximum_fusion.mk_ref
  5.0 10.2 %copy.8 = bf16[1536,4,384]{2,1,0:T(4,128)(2,1)} copy(bf16[1536,4,384]{0,1,2:T(4,128)(2,1)} %bitcast.18) | data formatting | bytes 9437184 | tf_op jit(solution)/shard_map/transpose | solution.py:469
  15.1 8.8 %reshape.45.a_ref = bf16[2,2,384,1536]{3,2,1,0:T(8,128)(2,1)} reshape(bf16[1536,4,384]{2,1,0:T(4,128)(2,1)} %copy.8) | data formatting | bytes 9437184 | tf_op jit(solution)/shard_map/reshape | solution.py:469
  23.9 8.9 %copy.9 = bf16[384,4,1536]{0,2,1:T(8,128)(2,1)} copy(bf16[384,4,1536]{2,1,0:T(4,128)(2,1)} %param.6) | data formatting | bytes 9437184 | tf_op args[1]
  32.8 8.4 %copy.10 = bf16[2,2,3,384,4,128]{5,4,3,2,1,0:T(4,128)(2,1)} copy(bf16[2,2,3,384,4,128]{3,5,2,1,0,4:T(8,128)(2,1)} %bitcast.19) | data formatting | bytes 9437184 | tf_op jit(solution)/shard_map/transpose | solution.py:468
  41.2 8.0 %reshape.47.c_ref = bf16[2,2,3,384,512]{4,3,2,1,0:T(8,128)(2,1)} reshape(bf16[2,2,3,384,4,128]{5,4,3,2,1,0:T(4,128)(2,1)} %copy.10) | data formatting | bytes 9437184 | tf_op jit(solution)/shard_map/reshape | solution.py:468
  49.3 356.7 %shard_map.55 = (bf16[2,384,1536]{2,1,0:T(8,128)(2,1)}, bf16[3,4,2,384,512]{4,3,2,1,0:T(8,128)(2,1)}, bf16[3,4,2,384,512]{4,3,2,1,0:T(8,128)(2,1)}) custom-call(bf16[2,384,1536]{2,1,0:T(8,128)(2,1)} %l_ref.1, bf16[2,2,384,1536]{3,2,1,0:T(8,128)(2,1)} %reshape.45.a_ref, bf16[2,2,3,384,512]{4,3,2,1,0:T(8,128)(2,1)} %reshape.47.c_ref, ...), custom_call_target="tpu_custom_call" | custom-call | tf_op jit(solution)/shard_map/pallas_call | solution.py:473
  406.0 3.2 copy.14
  (3 shorter events, 0.0 us)

commit v2 on v1

v2 whole, which is shorter than its diff:
```python
import functools

import jax
import jax.numpy as jnp
from jax import lax
from jax.experimental import pallas as pl
from jax.experimental.pallas import tpu as pltpu
from jax.sharding import PartitionSpec as P

K = 4
LANES = 128
MESH = pl.DeviceIdType.MESH
BF16 = jnp.bfloat16
F32 = jnp.float32


def mixing_of(block_values, pair_in, pair_out):
    comps = jnp.arange(K, dtype=jnp.int32)
    hot_out = (pair_out[:, None] == comps[None, :]).astype(F32)
    hot_in = (pair_in[:, None] == comps[None, :]).astype(F32)
    return jnp.einsum(
        "pv,pw,pst->vswt", hot_out, hot_in, block_values, precision=lax.Precision.HIGHEST
    )


def plain(left_env, site_tensor, block_values, pair_in, pair_out):
    rows_loc = left_env.shape[1]
    cols_loc = left_env.shape[2]
    phys = site_tensor.shape[1]
    mixing = mixing_of(block_values, pair_in, pair_out)
    splits = lax.axis_size("mpo")
    half_cols = cols_loc // splits
    own_start = lax.axis_index("mpo") * half_cols
    site_own = lax.dynamic_slice_in_dim(site_tensor, own_start, half_cols, 2)
    site_full = lax.all_gather(
        site_own.reshape(rows_loc, phys * half_cols), "bra", axis=0, tiled=True
    )
    piece = lax.all_gather(left_env, "ket", axis=2, tiled=True)
    piece = lax.all_gather(piece, "mpo", axis=0, tiled=True)
    comps_all, width = piece.shape[0], piece.shape[2]
    half = jnp.dot(
        piece.reshape(comps_all * rows_loc, width), site_full, preferred_element_type=F32
    )
    half = half.astype(BF16).reshape(comps_all, rows_loc, phys, half_cols)
    mixed = jnp.einsum(
        "vswt,watc->savc", mixing, half.astype(F32), precision=lax.Precision.HIGHEST
    ).astype(BF16)
    mixed_pairs = mixed.reshape(phys * rows_loc, comps_all * half_cols)
    site_wide = lax.all_gather(
        jnp.transpose(site_tensor, (1, 0, 2)), "ket", axis=2, tiled=True
    )
    site_pairs = site_wide.reshape(phys * rows_loc, site_wide.shape[2])
    term = lax.dot_general(
        site_pairs, mixed_pairs, (((0,), (0,)), ((), ())), preferred_element_type=F32
    ).astype(BF16)
    owned = lax.psum_scatter(term, "bra", scatter_dimension=0, tiled=True)
    owned = jnp.transpose(owned.reshape(-1, comps_all, half_cols), (1, 0, 2))
    return lax.all_to_all(owned, "mpo", split_axis=0, concat_axis=2, tiled=True)


def update_kernel(
    nz, nj, rows, phys,
    l_ref, s_ref, mix_ref,
    out_ref, up_ref, down_ref,
    env, conj, cols, half, terms, stage, raw, spread,
    own_sem, raw_sem, xy_send, xy_recv, col_send, col_recv, z_send, z_recv,
    up_send, up_recv, down_send, down_recv, stage_sem, fin_send, fin_recv, fin_own,
):
    bra, y, k = lax.axis_index("bra"), lax.axis_index("ket"), lax.axis_index("mpo")
    z, x = bra // 2, lax.rem(bra, 2)
    xo, yo, ko = 1 - x, 1 - y, 1 - k
    xn, yn, kn = (z * 2 + xo, y, k), (bra, yo, k), (bra, y, ko)
    xkn = (z * 2 + xo, y, ko)
    zu, zd = (bra + 2, y, k), (bra - 2, y, k)
    has_up, has_down = z < nz - 1, z > 0
    width = phys * LANES
    part = rows // 2

    barrier = pltpu.get_barrier_semaphore()
    for device in (xn, yn, kn, xkn):
        pl.semaphore_signal(barrier, inc=1, device_id=device, device_id_type=MESH)

    @pl.when(has_up)
    def _():
        pl.semaphore_signal(barrier, inc=1, device_id=zu, device_id_type=MESH)

    @pl.when(has_down)
    def _():
        pl.semaphore_signal(barrier, inc=1, device_id=zd, device_id_type=MESH)

    pl.semaphore_wait(barrier, 4 + (z + nz - 1) // nz + (2 * nz - 2 - z) // nz)

    def remote(src, dst, send, recv, device):
        return pltpu.make_async_remote_copy(
            src_ref=src, dst_ref=dst, send_sem=send, recv_sem=recv,
            device_id=device, device_id_type=MESH,
        )

    def slot(q, xs, ys, ks, h):
        if q == 0:
            return env.at[ys, xs, ks, h]
        return conj.at[2 * ys + lax.rem(h // 2 + ys, 2), xs, ks, pl.ds(h % 2 * part, part)]

    def own(q, h):
        return l_ref.at[h] if q == 0 else slot(1, x, y, k, h)

    def whole_over_y(q, h):
        return q == 0 and h == 0

    def xy(q, h, t, receiving):
        ks = ko if receiving else k
        size = part if q == 0 else part // 2
        upper, lower = pl.ds(0, size), pl.ds(size, size)
        if t == 0:
            dst = slot(q, xo if receiving else x, y, k, h)
            src, device = own(q, h), xn
        elif t == 1:
            dst = slot(q, x, yo if receiving else y, k, h)
            src, device = own(q, h), yn
        elif t == 2:
            dst = slot(q, xo if receiving else x, yo, k, h).at[lower]
            src, device = dst, xn
        elif t == 3:
            dst = slot(q, xo, yo if receiving else y, k, h)
            dst = dst if whole_over_y(q, h) else dst.at[upper]
            src, device = dst, yn
        else:
            dst = slot(q, xo if t in (5, 7) else x, yo if t in (6, 7) else y, ks, h)
            src, device = own(q, h) if t == 4 else dst, kn
        if receiving:
            src = dst
        return remote(src, dst, xy_send.at[q, h, t], xy_recv.at[q, h, t], device)

    def xy_start(q, h, t):
        xy(q, h, t, False).start()

    def xy_wait(q, h, t):
        xy(q, h, t, True).wait_recv()

    def from_x(q, h):
        xy_wait(q, h, 0)
        xy_start(q, h, 3)
        xy_start(q, h, 5)

    def from_y(q, h):
        xy_wait(q, h, 1)
        if not whole_over_y(q, h):
            xy_start(q, h, 2)
        xy_start(q, h, 6)

    def diagonal(q, h):
        if not whole_over_y(q, h):
            xy_wait(q, h, 2)
        xy_wait(q, h, 3)
        xy_start(q, h, 7)

    def from_core(q, h):
        for t in range(4 if q == 0 else 5, 8):
            xy_wait(q, h, t)

    def col_rows(index, count):
        return pl.ds(pl.multiple_of(index * rows, rows), count * rows)

    def col(j, receiving):
        dst = cols.at[j, col_rows(z * 2 + (xo if receiving else x), 1)]
        return remote(half.at[1, j], dst, col_send.at[j], col_recv.at[j], xn)

    def hop(j, up, s, receiving):
        piece = (z - s if receiving else z - s + 1) if up else (z + s if receiving else z + s - 1)
        ref = cols.at[j, col_rows(piece * 2, 2)]
        way = 0 if up else 1
        return remote(
            ref, ref, z_send.at[j, way, s - 1], z_recv.at[j, way, s - 1], zu if up else zd
        )

    def hop_sends(up, s):
        return (has_up & (z >= s - 1)) if up else (has_down & (z <= nz - s))

    def hop_start(j, s):
        for up in (True, False):
            @pl.when(hop_sends(up, s))
            def _():
                hop(j, up, s, False).start()

    def hop_sent(j):
        for s in range(1, nz):
            for up in (True, False):
                @pl.when(hop_sends(up, s))
                def _():
                    hop(j, up, s, False).wait_send()

    def hop_pass(j, s):
        for up in (True, False):
            @pl.when((z >= s) if up else (z < nz - s))
            def _():
                hop(j, up, s, True).wait_recv()

            if s < nz - 1:
                @pl.when(hop_sends(up, s + 1))
                def _():
                    hop(j, up, s + 1, False).start()

    deep = nz * rows

    def first_product(j, begin=0, end=4):
        def body(i, carry):
            xs, ks = i // 2, lax.rem(i, 2)
            acc = jnp.dot(
                env[0, xs, ks].reshape(2 * rows, deep), cols[j, :deep], preferred_element_type=F32
            )
            acc += jnp.dot(
                env[1, xs, ks].reshape(2 * rows, deep), cols[j, deep:], preferred_element_type=F32
            )
            half[xs, pl.ds(2 * ks, 2)] = acc.astype(BF16).reshape(2, rows, width)
            return carry

        lax.fori_loop(begin, end, body, 0)

    group = 4
    span = group * 16

    def mix(j):
        per_x = rows // span

        def body(i, carry):
            xs, base = i // per_x, pl.multiple_of(lax.rem(i, per_x) * span, span)
            tiles = [
                half[xs, w, pl.ds(base, span), t * LANES:(t + 1) * LANES]
                for w in range(K) for t in range(phys)
            ]
            right = jnp.concatenate(
                [
                    jnp.concatenate([tile[g * 16:(g + 1) * 16] for tile in tiles], axis=0)
                    for g in range(group)
                ],
                axis=1,
            )
            both = jnp.dot(spread[...], right, preferred_element_type=F32)
            size = K * phys * 16
            result = (both[:size] + both[size:]).astype(BF16)
            size = 16 * phys
            for v in range(K):
                for g in range(group):
                    at = pl.multiple_of(xs * deep + (base + g * 16) * phys, size)
                    cols[j, pl.ds(at, size), v * LANES:(v + 1) * LANES] = result[
                        v * size:(v + 1) * size, g * LANES:(g + 1) * LANES
                    ]
            return carry

        lax.fori_loop(0, 2 * per_x, body, 0)

    def term_ref(j, d, g):
        at = pl.ds(g * part, part)
        if j < 2:
            return terms.at[j, d, :, at]
        return env.at[d // 2, lax.rem(d, 2), 0, :, at, pl.ds((j - 2) * width, width)]

    def up_copy(j, d, g):
        return remote(
            term_ref(j, d, g), up_ref.at[j, d, :, pl.ds(g * part, part)],
            up_send.at[j, d, g], up_recv.at[j, d, g], zu,
        )

    def down_copy(j, d, g):
        return remote(
            term_ref(j, d, g), down_ref.at[j, d, :, pl.ds(g * part, part)],
            down_send.at[j, d, g], down_recv.at[j, d, g], zd,
        )

    def second_product(j, d, g, ups=True, downs=True):
        out = term_ref(j, d, g)
        at = slice(g * part, (g + 1) * part)
        acc = jnp.dot(
            conj[d, 0, :, at].reshape(rows, deep), cols[j, :deep], preferred_element_type=F32
        )
        acc += jnp.dot(
            conj[d, 1, :, at].reshape(rows, deep), cols[j, deep:], preferred_element_type=F32
        )
        out[...] = acc.astype(BF16).reshape(2, part, width)
        if ups:
            @pl.when(z == 0)
            def _():
                up_copy(j, d, g).start()
        if downs:
            @pl.when(z == nz - 1)
            def _():
                down_copy(j, d, g).start()

    def far_products(j, g):
        second_product(j, nz - 1, g, downs=False)
        second_product(j, 0, g, ups=False)

    strip = part // 2
    strips = part // strip

    def strip_of(i):
        return i // strips, pl.ds(pl.multiple_of(lax.rem(i, strips) * strip, strip), strip)

    def fetch(src, index):
        return pltpu.make_async_copy(src, stage.at[index], stage_sem.at[index])

    def landed(ref, j, d, g):
        return ref.at[j, d, :, pl.ds(g * part, part)]

    def pass_on(j, d, g, up):
        copy = up_copy(j, d, g) if up else down_copy(j, d, g)
        copy.wait_recv()
        local = fetch(landed(up_ref if up else down_ref, j, d, g), 0)
        local.start()
        local.wait()
        ref = term_ref(j, d, g)

        def body(i, carry):
            b, r = strip_of(i)
            ref[b, r] = (ref[b, r].astype(F32) + stage[0, b, r].astype(F32)).astype(BF16)
            return carry

        lax.fori_loop(0, 2 * strips, body, 0)
        copy.start()

    def place(block, j, g):
        at = pl.multiple_of((block * nj + j) * LANES, LANES)
        return out_ref.at[:, pl.ds(g * part, part), pl.ds(at, LANES)]

    def summed(xs, ks, j, g):
        at = slice(j * LANES, (j + 1) * LANES)
        return half.at[xs, pl.ds(2 * ks, 2), pl.ds(g * part, part), at]

    def fin(j, g, t, receiving):
        xs, ks, device = ((x, ko, kn), (xo, k, xn), (xo, ko, xkn))[t]
        dst = place((xs * 2 + ks) if receiving else (x * 2 + k), j, g)
        return remote(
            summed(xs, ks, j, g), dst, fin_send.at[j, g, t], fin_recv.at[j, g, t], device
        )

    def fin_local(j, g):
        return pltpu.make_async_copy(
            summed(x, k, j, g), place(x * 2 + k, j, g), fin_own.at[j, g]
        )

    def finish(j, d, g):
        below, above = d > 0, d < nz - 1
        count = 0
        for there, copy, src in ((below, up_copy, up_ref), (above, down_copy, down_ref)):
            if there:
                copy(j, d, g).wait_recv()
                fetch(landed(src, j, d, g), count).start()
                count += 1
        for index in range(count):
            fetch(landed(up_ref, j, d, g), index).wait()
        ref = term_ref(j, d, g)

        def body(i, carry):
            b, r = strip_of(i)
            value = ref[b, r].astype(F32)
            for index in range(count):
                value += stage[index, b, r].astype(F32)
            value = value.astype(BF16)
            at = pl.ds(pl.multiple_of(g * part + lax.rem(i, strips) * strip, strip), strip)
            for v in range(K):
                half[b, v, at, j * LANES:(j + 1) * LANES] = value[:, v * LANES:(v + 1) * LANES]
            return carry

        lax.fori_loop(0, 2 * strips, body, 0)
        for t in (1, 2, 0):
            fin(j, g, t, False).start()
        fin_local(j, g).start()

    deal = 64
    deals = rows // deal
    lump = deal * phys

    def load(i):
        at = pl.ds(i * deal, deal)
        return pltpu.make_async_copy(s_ref.at[at], raw.at[i % 2], raw_sem.at[i % 2])

    def each_deal(work):
        load(0).start()
        for i in range(deals):
            if i + 1 < deals:
                load(i + 1).start()
            load(i).wait()
            work(i)

    row_id = lax.broadcasted_iota(jnp.int32, (lump, lump), 0)
    col_id = lax.broadcasted_iota(jnp.int32, (lump, lump), 1)
    wanted = (row_id & (deal - 1)) * phys + row_id // deal
    permute = (col_id == wanted).astype(F32).astype(BF16)

    def to_cols(i):
        for xs in (xo, x):
            at = pl.ds(pl.multiple_of((xs * 2 + k) * nj * LANES, LANES), nj * LANES)
            piece = raw[i % 2, :, :, at].reshape(lump, nj * LANES)
            piece = jnp.dot(permute, piece, preferred_element_type=F32).astype(BF16)
            for j in range(nj):
                for t in range(phys):
                    tile = piece[t * deal:(t + 1) * deal, j * LANES:(j + 1) * LANES]
                    lanes = slice(t * LANES, (t + 1) * LANES)
                    if xs is xo:
                        half[1, j, i * deal:(i + 1) * deal, lanes] = tile
                    else:
                        base = pl.multiple_of((z * 2 + x) * rows + i * deal, deal)
                        cols[j, pl.ds(base, deal), lanes] = tile

    def to_conj(i):
        for dl in range(2):
            for kk in range(2):
                at = (dl * 2 + kk) * rows
                piece = raw[i % 2, :, :, at:at + rows].reshape(lump, rows)
                conj[2 * y + dl, x, kk, :, i * lump:(i + 1) * lump] = piece.T

    def make_spread():
        pairs, size = K * phys, K * phys * 16
        ids = lambda shape, dim: lax.broadcasted_iota(jnp.int32, shape, dim)
        one_hot = lambda match: match.astype(F32).astype(BF16)
        out, kind = ids((size, pairs), 0), ids((size, pairs), 1)
        left = one_hot(out // (16 * phys) * phys + (out & (phys - 1)) == kind)
        kind, into = ids((pairs, size), 0), ids((pairs, size), 1)
        right = one_hot(into // 16 == kind)
        out, into = ids((size, size), 0), ids((size, size), 1)
        same = ((out // phys) & 15) == (into & 15)
        high = mix_ref[...].astype(BF16)
        low = (mix_ref[...] - high.astype(F32)).astype(BF16)
        for index, value in enumerate((high, low)):
            rows_of = jnp.dot(left, value, preferred_element_type=F32).astype(BF16)
            full = jnp.dot(rows_of, right, preferred_element_type=F32)
            full = jnp.where(same, full, 0.0).astype(BF16)
            spread[index * size:(index + 1) * size] = full

    for h in range(2):
        xy_start(0, h, 1)
        xy_start(0, h, 4)
    env_own = [
        pltpu.make_async_copy(l_ref.at[h], env.at[y, x, k, h], own_sem.at[h]) for h in range(2)
    ]
    each_deal(to_cols)
    for j in range(nj):
        col(j, False).start()
    for h in range(2):
        xy_start(0, h, 0)
    for copy in env_own:
        copy.start()
    each_deal(to_conj)
    make_spread()

    def hop_first(j):
        col(j, True).wait_recv()
        hop_start(j, 1)

    hop_first(0)
    from_y(0, 0)
    hop_pass(0, 1)
    from_y(0, 1)
    hop_pass(0, 2)
    hop_first(1)
    from_x(0, 0)
    hop_pass(0, 3)
    hop_pass(1, 1)
    from_x(0, 1)
    xy_start(1, 0, 0)
    xy_start(1, 0, 1)
    hop_pass(1, 2)
    for j in range(2, nj):
        hop_first(j)
    diagonal(0, 0)
    diagonal(0, 1)
    for copy in env_own:
        copy.wait()
    for j in range(nj):
        col(j, False).wait_send()
    from_core(0, 0)
    from_core(0, 1)

    waiting = [[] for _ in range(nz)]

    def reduce(order, last=False):
        for own_z in range(nz):
            tasks = []
            for j, d, g in order:
                d = d if 2 * own_z < nz else nz - 1 - d
                if d == own_z and not last:
                    waiting[own_z].append((j, d, g))
                else:
                    tasks.append((j, d, g))
            if last:
                tasks = waiting[own_z] + tasks

            @pl.when(z == own_z)
            def _():
                for j, d, g in tasks:
                    if d == own_z:
                        finish(j, d, g)
                    elif d > own_z and own_z > 0:
                        pass_on(j, d, g, True)
                    elif d < own_z and own_z < nz - 1:
                        pass_on(j, d, g, False)

    second = nz - 2 - z // 2
    third = 1 + z // 2
    late = range(2, nj)

    first_product(0, 0, 2)
    from_y(1, 0)
    from_x(1, 0)
    for h in (1, 2):
        xy_start(1, h, 0)
        xy_start(1, h, 1)
    first_product(0, 2, 4)
    hop_sent(0)
    mix(0)
    diagonal(1, 0)
    from_core(1, 0)
    far_products(0, 0)
    hop_pass(1, 3)
    first_product(1, 0, 2)
    from_y(1, 1)
    from_x(1, 1)
    xy_start(1, 3, 0)
    xy_start(1, 3, 1)
    first_product(1, 2, 4)
    hop_sent(1)
    mix(1)
    far_products(1, 0)
    for j in late:
        hop_pass(j, 1)
    reduce([(0, 3, 0)])
    diagonal(1, 1)
    from_core(1, 1)
    far_products(0, 1)
    far_products(1, 1)
    from_y(1, 2)
    from_x(1, 2)
    for j in late:
        hop_pass(j, 2)
    reduce([(1, 3, 0)])
    from_y(1, 3)
    from_x(1, 3)
    diagonal(1, 2)
    from_core(1, 2)
    second_product(0, second, 0)
    second_product(1, second, 0)
    reduce([(0, 3, 1), (1, 3, 1)])
    diagonal(1, 3)
    from_core(1, 3)
    second_product(0, second, 1)
    second_product(1, second, 1)
    reduce([(0, 0, 0), (1, 0, 0), (0, 2, 0)])
    for j in late:
        hop_pass(j, 3)
        first_product(j)
        hop_sent(j)
        mix(j)
    for h in range(2):
        for t in range(8):
            if t != 2 or not whole_over_y(0, h):
                xy(0, h, t, False).wait_send()
    for j in late:
        for g in range(2):
            far_products(j, g)
    reduce([(1, 2, 0), (0, 0, 1), (1, 0, 1), (0, 2, 1)])
    for j in late:
        for g in range(2):
            second_product(j, second, g)
    for j in range(nj):
        for g in range(2):
            second_product(j, third, g)
    rest = [(1, 2, 1)]
    for j in late:
        rest += [(j, 3, 0), (j, 3, 1), (j, 2, 0), (j, 0, 0), (j, 2, 1), (j, 0, 1)]
    reduce(rest + [(j, 1, g) for j in range(nj) for g in range(2)], last=True)
    for own_z in range(nz):
        @pl.when(z == own_z)
        def _():
            for j in range(nj):
                for g in range(2):
                    for d in range(nz):
                        if d > own_z:
                            up_copy(j, d, g).wait_send()
                        elif d < own_z:
                            down_copy(j, d, g).wait_send()

    for j in range(nj):
        for g in range(2):
            fin_local(j, g).wait()
            for t in range(3):
                fin(j, g, t, False).wait_send()
                fin(j, g, t, True).wait_recv()
    for h in range(4):
        for t in (0, 1, 2, 3, 5, 6, 7):
            xy(1, h, t, False).wait_send()


def fused(nz, left_env, site_tensor, block_values, pair_in, pair_out):
    rows, phys, width_loc = site_tensor.shape
    nj = width_loc // (4 * LANES)
    mixing = mixing_of(block_values, pair_in, pair_out).reshape(K * phys, K * phys)
    width = phys * LANES
    dma = pltpu.SemaphoreType.DMA
    anywhere = pl.BlockSpec(memory_space=pl.ANY)
    out, _, _ = pl.pallas_call(
        functools.partial(update_kernel, nz, nj, rows, phys),
        out_shape=(
            jax.ShapeDtypeStruct(left_env.shape, BF16),
            jax.ShapeDtypeStruct((nj, nz, 2, rows, width), BF16),
            jax.ShapeDtypeStruct((nj, nz, 2, rows, width), BF16),
        ),
        in_specs=[anywhere, anywhere, pl.BlockSpec(memory_space=pltpu.VMEM)],
        out_specs=(anywhere, anywhere, anywhere),
        scratch_shapes=[
            pltpu.VMEM((2, 2, 2, 2, rows, width_loc), BF16),
            pltpu.VMEM((nz, 2, 2, rows, rows * phys), BF16),
            pltpu.VMEM((nj, 2 * nz * rows, width), BF16),
            pltpu.VMEM((2, K, rows, width), BF16),
            pltpu.VMEM((2, nz, 2, rows, width), BF16),
            pltpu.VMEM((2, 2, rows // 2, width), BF16),
            pltpu.VMEM((2, 64, phys, width_loc), BF16),
            pltpu.VMEM((2 * K * phys * 16, K * phys * 16), BF16),
            dma((2,)), dma((2,)),
            dma((2, 4, 8)), dma((2, 4, 8)),
            dma((nj,)), dma((nj,)),
            dma((nj, 2, nz - 1)), dma((nj, 2, nz - 1)),
            dma((nj, nz, 2)), dma((nj, nz, 2)),
            dma((nj, nz, 2)), dma((nj, nz, 2)),
            dma((2,)),
            dma((nj, 2, 3)), dma((nj, 2, 3)), dma((nj, 2)),
        ],
        compiler_params=pltpu.CompilerParams(
            collective_id=0, has_side_effects=True, vmem_limit_bytes=67043328
        ),
    )(left_env, site_tensor, mixing)
    return out


def solution(mesh):
    sizes = dict(mesh.shape)

    def local(left_env, site_tensor, block_values, pair_in, pair_out):
        comps_loc = left_env.shape[0]
        rows, phys, width = site_tensor.shape
        fits = (
            sizes["ket"] == 2 and sizes["mpo"] == 2 and sizes["bra"] == 8
            and comps_loc == 2 and phys == 4 and rows % 192 == 0
            and width == (sizes["bra"] // 2) * rows and width % (4 * LANES) == 0
            and 2 <= width // (4 * LANES) <= 3 and rows <= 384
        )
        if fits:
            return fused(
                sizes["bra"] // 2, left_env, site_tensor, block_values, pair_in, pair_out
            )
        return plain(left_env, site_tensor, block_values, pair_in, pair_out)

    return jax.shard_map(
        local,
        mesh=mesh,
        in_specs=(P("mpo", "bra", "ket"), P("bra", None, "ket"), P(), P(), P()),
        out_specs=P("mpo", "bra", "ket"),
        check_vma=False,
    )
```

time: 411 us -> 314 us (0.76)
  Pallas kernels: 357 us -> 306 us
  local copies, waits for them, and re-layouts: 49.6 us -> 3.92 us
    pallas_call x1, Pallas kernels: 357 us -> 306 us  [fused(): pl.pallas_call(functools.partial(update_kernel, nz, nj, rows, phys), out_...]
    transpose x2 -> x0, local copies, waits for them, and re-layouts: 18.5 us -> none  [the longest x1 10.2 us: fused(): turned = site_tensor.transpose(2, 1, 0).reshape(2, 2, rows, phys * rows)]
    reshape x2 -> x0, local copies, waits for them, and re-layouts: 16.8 us -> none  [the longest x1 8.76 us: fused(): turned = site_tensor.transpose(2, 1, 0).reshape(2, 2, rows, phys * rows)]
    unnamed x2 -> x1, local copies, waits for them, and re-layouts: 12.2 us -> 3.22 us
where the time goes in v2:
time: 314 us; the launch traced here: 312 us
  Pallas kernels  306 us (97%)
  local copies, waits for them, and re-layouts  3.92 us (1%)
    pallas_call x1, Pallas kernels, fused(): pl.pallas_call(functools.partial(update_kernel, nz, nj, rows, phys), out_...  306 us

profile of v2, /device:TPU:12, one launch (start us, length us, event | category | flops | bytes accessed | tf_op | source)
XLA Modules:
  0.0 311.7 jit_solution(15908376656829841617)
XLA Ops:
  0.0 0.7 fusion.5
  0.7 1.0 convolution_bitcast_fusion
  1.7 0.7 reshape.5.mix_ref
  2.4 306.0 %shard_map.55 = (bf16[2,384,1536]{2,1,0:T(8,128)(2,1)}, bf16[3,4,2,384,512]{4,3,2,1,0:T(8,128)(2,1)}, bf16[3,4,2,384,512]{4,3,2,1,0:T(8,128)(2,1)}) custom-call(bf16[2,384,1536]{2,1,0:T(8,128)(2,1)} %l_ref.1, bf16[384,4,1536]{2,1,0:T(4,128)(2,1)} %s_ref.1, f32[16,16]{1,0:T(8,128)} %reshape.5.mix_ref), custom_call_target="tpu_custom_call" | custom-call | tf_op jit(solution)/shard_map/pallas_call | solution.py:600
  308.5 3.2 %copy.9 = bf16[2,384,1536]{2,1,0:T(8,128)(2,1)} copy(bf16[2,384,1536]{2,1,0:T(8,128)(2,1)} %get-tuple-element.6) | data formatting | bytes 4718592
  (1 shorter events, 0.0 us)
